TPU v7x, 32 devices: a whole 2x2x4 slice. The times are simulated.
32 devices in a mesh: dp: 4 (over x, y), ep: 8 (over z, core).
Axes of the slice: x: 2, y: 2, z: 4, core: 2. Of those that a mesh axis runs over, the one named last changes fastest.
Arguments:
- hidden: bfloat16 [65536, 2048], P(('dp', 'ep')), parts along dimension 0
- ln_gamma: float32 [2048], replicated
- ln_beta: float32 [2048], replicated
- w_router: bfloat16 [2048, 8], replicated
- w_gate: bfloat16 [8, 2048, 5632], P('ep')
- w_up: bfloat16 [8, 2048, 5632], P('ep')
- w_down: bfloat16 [8, 5632, 2048], P('ep')
- choice: int32 [65536, 2], P(('dp', 'ep')), parts along dimension 0
- mask_first: int32 [65536, 8], P(('dp', 'ep')), parts along dimension 0
- mask_second: int32 [65536, 8], P(('dp', 'ep')), parts along dimension 0
Outputs:
- output: bfloat16 [65536, 2048], P(('dp', 'ep')), parts along dimension 0
There are 4 independent parts. A program takes and returns all parts, laid end to end along the dimension named above; an argument that names none is the same for every part.
All inputs are finite; a program needn't handle non-finite values.
Results may differ from a plain program's by a relative error of at most 0.00104.
Values are sent between devices in bfloat16 or wider.
A program may use at most 1 GiB of HBM per device.

v0:
```python
import jax
import jax.numpy as jnp
from jax import lax
from jax.sharding import PartitionSpec as P

LN_EPS = 1e-5


def layer_norm(token_rows, ln_gamma, ln_beta):
    values = token_rows.astype(jnp.float32)
    centred = values - jnp.mean(values, axis=-1, keepdims=True)
    variance = jnp.mean(centred * centred, axis=-1, keepdims=True)
    return (centred * lax.rsqrt(variance + LN_EPS) * ln_gamma + ln_beta).astype(jnp.bfloat16)


def sparse_gates(normed, w_router, choice, mask_first, mask_second):
    scores = jnp.dot(normed, w_router, preferred_element_type=jnp.float32)
    expert_ids = jnp.arange(w_router.shape[1], dtype=jnp.int32)
    mask_pair = jnp.stack([mask_first, mask_second], axis=1) > 0
    soft_probs = jax.nn.softmax(jnp.where(mask_pair, scores[:, None, :], -jnp.inf), axis=-1)
    return jnp.sum(jnp.where(choice[:, :, None] == expert_ids, soft_probs, 0.0), axis=-1)


def copy_slots(choice, experts, capacity):
    expert_ids = jnp.arange(experts, dtype=jnp.int32)
    hit_count = (choice[..., None] == expert_ids).astype(jnp.int32)
    per_token = jnp.sum(hit_count, axis=-2)
    before = jnp.cumsum(per_token, axis=-2) - per_token
    position = jnp.sum(hit_count * before[..., None, :], axis=-1)
    return position, position < capacity


def expert_mlp(expert_in, w_gate, w_up, w_down):
    gate_proj = jnp.einsum("secd,edf->secf", expert_in, w_gate, preferred_element_type=jnp.float32)
    up_proj = jnp.einsum("secd,edf->secf", expert_in, w_up, preferred_element_type=jnp.float32)
    inner_act = (jax.nn.silu(gate_proj) * up_proj).astype(jnp.bfloat16)
    return jnp.einsum("secf,efd->secd", inner_act, w_down, preferred_element_type=jnp.float32).astype(jnp.bfloat16)


def solution(mesh):
    group_size = mesh.shape["ep"]
    rows_spec = P(("dp", "ep"))

    def device_step(hidden, ln_gamma, ln_beta, w_router, w_gate, w_up, w_down, choice, mask_first, mask_second):
        tokens, row_width = hidden.shape
        local_experts = w_gate.shape[0]
        experts = local_experts * group_size
        capacity = (10 * tokens + 4 * experts - 1) // (4 * experts)
        slot_count = experts * capacity
        normed = layer_norm(hidden, ln_gamma, ln_beta)
        gate_vals = sparse_gates(normed, w_router, choice, mask_first, mask_second)
        position, kept_copy = copy_slots(choice, experts, capacity)
        flat_slot = jnp.where(kept_copy, choice * capacity + position, slot_count)
        token_ids = jnp.broadcast_to(jnp.arange(tokens, dtype=jnp.int32)[:, None], (tokens, 2))
        source_row = jnp.full((slot_count,), tokens, jnp.int32).at[flat_slot.reshape(-1)].set(token_ids.reshape(-1), mode="drop")
        send_rows = jnp.take(normed, source_row, axis=0, mode="fill", fill_value=0)
        recv_rows = lax.all_to_all(send_rows, "ep", 0, 0, tiled=True)
        expert_out = expert_mlp(recv_rows.reshape(group_size, local_experts, capacity, row_width), w_gate, w_up, w_down)
        back_rows = lax.all_to_all(expert_out.reshape(slot_count, row_width), "ep", 0, 0, tiled=True)
        picked = jnp.take(back_rows, flat_slot, axis=0, mode="fill", fill_value=0)
        mixed_out = hidden.astype(jnp.float32) + jnp.sum(gate_vals[:, :, None] * picked.astype(jnp.float32), axis=1)
        return mixed_out.astype(jnp.bfloat16)

    return jax.shard_map(device_step, mesh=mesh,
                         in_specs=(rows_spec, P(), P(), P(), P("ep"), P("ep"), P("ep"), rows_spec, rows_spec, rows_spec),
                         out_specs=rows_spec, check_vma=False)
```

profile of v0, /device:TPU:0, one launch (start us, length us, event | category | flops | bytes accessed | tf_op | source)
XLA Modules:
  0.0 1570.4 jit_solution(1991883451660014246)
XLA Ops:
  0.0 0.0 copy-start
  0.0 0.0 copy-start.5
  0.0 0.0 copy-start.6
  0.0 0.8 convert_reduce_fusion.1
  0.8 2.3 reduce-window.6
  3.1 0.3 slice_reduce_fusion
  3.4 0.2 reduce-window.9
  3.5 0.1 add_bitcast_fusion
  3.7 0.8 select_reduce_fusion.1
  4.5 1.3 compare_and_fusion
  5.8 0.0 copy-start.1
  5.8 0.4 copy.17
  6.2 0.6 reshape.110
  6.8 0.1 broadcast_in_dim.75
  6.9 0.5 reshape.136
  7.4 15.5 scatter_custom_fusion
  23.0 4.5 convert_reduce_fusion
  27.5 5.7 fusion.18
  33.3 0.0 copy-done.5
  33.3 0.0 copy-done.6
  33.3 8.6 fusion.21
  41.9 43.3 %gather_fusion = bf16[5120,2048]{1,0:T(8,128)(2,1)} fusion(bf16[2048,2048]{1,0:T(8,128)(2,1)} %fusion.21, s32[5120]{0:T(1024)S(1)} %fusion.38), kind=kCustom, calls=%fused_computation | custom fusion | bytes 41963520 | tf_op jit(solution)/shard_map/jit(_take)/gather | solution.py:56
  85.2 0.0 copy-done.1
  85.2 10.3 broadcast_select_fusion.1
  95.5 461.7 %all_to_all.15 = bf16[8,640,2048]{2,1,0:T(8,128)(2,1)} all-to-all(bf16[8,640,2048]{2,1,0:T(8,128)(2,1)S(1)} %broadcast_select_fusion.1), channel_id=1, replica_groups=mesh['dp'=4,'ep'=8] {'ep'}, dimensions={0} | all-to-all | bytes 41943040 | tf_op jit(solution)/shard_map/all_to_all | solution.py:57
  557.1 130.6 %fusion.14 = f32[8,640,5632]{2,1,0:T(8,128)} fusion(bf16[8,640,2048]{2,1,0:T(8,128)(2,1)} %all_to_all.15, bf16[1,2048,5632]{2,1,0:T(8,128)(2,1)} %param.14), kind=kOutput, calls=%fused_computation.22 | convolution fusion | flops 118111600640 | bytes 159383552 | tf_op jit(solution)/shard_map/secd,edf->secf/dot_general | solution.py:34
  687.8 136.1 %fusion.64 = bf16[8,640,5632]{2,1,0:T(8,128)(2,1)} fusion(f32[8,640,5632]{2,1,0:T(8,128)} %fusion.14, bf16[8,640,2048]{2,1,0:T(8,128)(2,1)} %all_to_all.15, bf16[1,2048,5632]{2,1,0:T(8,128)(2,1)} %param.15), kind=kOutput, calls=%fused_computation.13.clone.clone.clone.1 | convolution fusion | flops 118284615680 | bytes 217055232 | tf_op jit(solution)/shard_map/secd,edf->secf/dot_general | solution.py:35
  823.8 129.6 %fusion.23 = bf16[8,640,2048]{2,1,0:T(8,128)(2,1)} fusion(bf16[1,5632,2048]{2,1,0:T(8,128)(2,1)} %param.16, bf16[8,640,5632]{2,1,0:T(8,128)(2,1)} %fusion.64), kind=kOutput, calls=%fused_computation.32 | convolution fusion | flops 118122086400 | bytes 101711872 | tf_op jit(solution)/shard_map/secf,efd->secd/dot_general | solution.py:37
  953.5 0.0 copy-start.4
  953.5 0.0 copy-start.2
  953.5 0.0 copy-start.3
  953.5 0.0 copy-start.7
  953.5 0.0 copy-start.8
  953.5 6.5 all-to-all-start.1
  960.0 0.0 copy-done.4
  960.0 0.5 copy.16
  960.5 0.0 copy-done.2
  960.5 0.4 copy.18
  960.9 0.5 reshape.126
  961.4 0.0 copy-done
  961.4 5.6 fusion.50
  967.0 0.0 copy-done.3
  967.0 0.0 copy-done.7
  967.0 0.0 copy-done.8
  967.1 0.1 fusion.47
  967.2 0.4 copy.15
  967.6 445.6 %all-to-all-done.1 = bf16[8,640,2048]{2,1,0:T(8,128)(2,1)} async-done(((bf16[8,640,2048]{2,1,0:T(8,128)(2,1)}), bf16[8,640,2048]{2,1,0:T(8,128)(2,1)}, u32[]{:S(2)}, u32[]{:S(2)}) %all-to-all-start.1) | async-done | bytes 20971552 | tf_op jit(solution)/shard_map/all_to_all | solution.py:59
  1413.2 41.0 %gather_fusion.1 = bf16[4096,2048]{1,0:T(8,128)(2,1)} fusion(bf16[5120,2048]{1,0:T(8,128)(2,1)} %bitcast.21, s32[4096]{0:T(1024)S(1)} %broadcast_clamp_fusion), kind=kCustom, calls=%fused_computation.1 | custom fusion | bytes 33570816 | tf_op jit(solution)/shard_map/jit(_take)/gather | solution.py:60
  1454.2 27.0 %reshape.125 = bf16[2048,2,2048]{2,1,0:T(2,128)(2,1)} reshape(bf16[4096,2048]{1,0:T(8,128)(2,1)} %gather_fusion.1) | data formatting | bytes 33554432 | tf_op jit(solution)/shard_map/jit(_take)/gather | solution.py:60
  1481.2 76.8 %multiply_reduce_fusion = f32[2048,2048]{1,0:T(8,128)} fusion(bf16[2048,2,2048]{2,1,0:T(2,128)(2,1)} %reshape.125, pred[2048,2]{1,0:T(8,128)(4,1)S(1)} %copy.16, f32[2048,2]{1,0:T(8,128)S(1)} %copy.15), kind=kLoop, calls=%fused_computation.15 | loop fusion | flops 29360128 | bytes 33574912 | tf_op jit(solution)/shard_map/reduce_sum | solution.py:61
  1558.0 12.0 fusion.22
  (10 shorter events, 0.1 us)
Async XLA Ops:
  0.0 961.4 %copy-start = (bf16[2048,8]{0,1:T(8,128)(2,1)S(1)}, bf16[2048,8]{0,1:T(8,128)(2,1)}, u32[]{:S(2)}) copy-start(bf16[2048,8]{0,1:T(8,128)(2,1)} %param.13) | copy-start | bytes 98308
  0.0 33.3 %copy-start.5 = (f32[2048]{0:T(1024)S(1)}, f32[2048]{0:T(1024)}, u32[]{:S(2)}) copy-start(f32[2048]{0:T(1024)} %param.12) | copy-start | bytes 24580
  0.0 33.3 %copy-start.6 = (f32[2048]{0:T(1024)S(1)}, f32[2048]{0:T(1024)}, u32[]{:S(2)}) copy-start(f32[2048]{0:T(1024)} %param.11) | copy-start | bytes 24580
  5.8 79.4 %copy-start.1 = (s32[2048,2]{0,1:T(2,128)}, s32[2048,2]{0,1:T(2,128)S(1)}, u32[]{:S(2)}) copy-start(s32[2048,2]{0,1:T(2,128)S(1)} %get-tuple-element.6) | copy-start | bytes 49156
  953.5 6.5 copy-start.4
  953.5 7.0 copy-start.2
  953.5 13.5 copy-start.3
  953.5 13.5 copy-start.7
  953.5 13.5 copy-start.8
  953.5 459.7 %all-to-all-start.1 = ((bf16[8,640,2048]{2,1,0:T(8,128)(2,1)}), bf16[8,640,2048]{2,1,0:T(8,128)(2,1)}, u32[]{:S(2)}, u32[]{:S(2)}) async-start(bf16[8,640,2048]{2,1,0:T(8,128)(2,1)} %fusion.23), calls=%async_computation.1 | async-start | bytes 41943040 | tf_op jit(solution)/shard_map/all_to_all | solution.py:59
where the time goes:
time: 1580 us; the launch traced here: 1570 us
  blocking collectives  462 us (29%)
  waiting for transfers between devices  446 us (28%)
  matrix products  402 us (25%)
  local copies, waits for them, and re-layouts  130 us (8%)
  other arithmetic  124 us (8%)
    all_to_all x1, blocking collectives, device_step(): recv_rows = lax.all_to_all(send_rows, 'ep', 0, 0, tiled=True)  462 us
    all_to_all x1, waiting for transfers between devices, device_step(): lax.all_to_all(expert_out.reshape(slot_count, row_width), 'ep', 0, 0, til...  446 us
    dot_general x1, matrix products, expert_mlp(): jnp.einsum('secd,edf->secf', expert_in, w_up, preferred_element_type=jnp....  136 us
    dot_general x1, matrix products, expert_mlp(): jnp.einsum('secd,edf->secf', expert_in, w_gate, preferred_element_type=jn...  131 us
    dot_general x1, matrix products, expert_mlp(): jnp.einsum('secf,efd->secd', inner_act, w_down, preferred_element_type=jn...  130 us
    reduce_sum x1, other arithmetic, device_step(): jnp.sum(gate_vals[:, :, None] * picked.astype(jnp.float32), axis=1)  76.8 us
    gather x2, local copies, waits for them, and re-layouts, device_step(): picked = jnp.take(back_rows, flat_slot, axis=0, mode='fill', fill_value=0)  68 us
    gather x1, local copies, waits for them, and re-layouts, device_step(): send_rows = jnp.take(normed, source_row, axis=0, mode='fill', fill_value=0)  43.3 us
  transfers between devices with their start and end apart: 1, of which 1 were waited for; matrix products, arithmetic and copies ran while one was open for 0% of the time, Pallas kernels for 0%

commit v1 on v0

v1 whole, which is shorter than its diff:
```python
import functools

import jax
import jax.numpy as jnp
from jax import lax
from jax.experimental import pallas as pl
from jax.experimental.pallas import tpu as pltpu
from jax.sharding import PartitionSpec as P

LN_EPS = 1e-5
MESH = pl.DeviceIdType.MESH


def layer_norm(token_rows, ln_gamma, ln_beta):
    values = token_rows.astype(jnp.float32)
    centred = values - jnp.mean(values, axis=-1, keepdims=True)
    variance = jnp.mean(centred * centred, axis=-1, keepdims=True)
    return (centred * lax.rsqrt(variance + LN_EPS) * ln_gamma + ln_beta).astype(jnp.bfloat16)


def sparse_gates(normed, w_router, choice, mask_first, mask_second):
    scores = jnp.dot(normed, w_router, preferred_element_type=jnp.float32)
    expert_ids = jnp.arange(w_router.shape[1], dtype=jnp.int32)
    mask_pair = jnp.stack([mask_first, mask_second], axis=1) > 0
    soft_probs = jax.nn.softmax(jnp.where(mask_pair, scores[:, None, :], -jnp.inf), axis=-1)
    return jnp.sum(jnp.where(choice[:, :, None] == expert_ids, soft_probs, 0.0), axis=-1)


def xor(a, b, n):
    total, bit = 0, 1
    while bit < n:
        p, q = (a // bit) % 2, (b // bit) % 2
        total = total + bit * (p + q - 2 * p * q)
        bit *= 2
    return total


def visit(i):
    return i + (i // 4) * (2 - 4 * ((i // 2) % 2))


def moe_kernel(n, cap, ft, tc, pos_row, pos_col, gate_col, u_hbm, x_hbm, wg, wu, wd,
               out, sbuf, rbuf, ybuf, bbuf,
               ubuf, pmat, temp, xin, acc, wgb, wub, wdb, oacc,
               send_sem, recv_sem, ysend_sem, yrecv_sem, wsem, lsem, osem):
    me = lax.axis_index("ep")
    tokens, width = ubuf.shape
    nf = wg.shape[1] // ft
    ncol = width // 512
    bf16, f32 = jnp.bfloat16, jnp.float32

    u_copy = pltpu.make_async_copy(u_hbm, ubuf, lsem.at[0])
    u_copy.start()

    def weight_copies(f, slot):
        cols = pl.ds(pl.multiple_of(f * ft, ft), ft)
        return (pltpu.make_async_copy(wg.at[:, cols], wgb.at[slot], wsem.at[slot, 0]),
                pltpu.make_async_copy(wu.at[:, cols], wub.at[slot], wsem.at[slot, 1]),
                pltpu.make_async_copy(wd.at[cols, :], wdb.at[slot], wsem.at[slot, 2]))

    for c in weight_copies(0, 0):
        c.start()

    barrier = pltpu.get_barrier_semaphore()

    def greet(k, _):
        pl.semaphore_signal(barrier, inc=1, device_id={"ep": xor(me, k, n)}, device_id_type=MESH)
        return 0

    lax.fori_loop(1, n, greet, 0)
    pl.semaphore_wait(barrier, n - 1)
    u_copy.wait()

    def send_copy(k):
        return pltpu.make_async_remote_copy(
            src_ref=sbuf.at[k], dst_ref=rbuf.at[k], send_sem=send_sem.at[k], recv_sem=recv_sem.at[k],
            device_id={"ep": xor(me, k, n)}, device_id_type=MESH)

    def back_copy(k):
        return pltpu.make_async_remote_copy(
            src_ref=ybuf.at[k], dst_ref=bbuf.at[k], send_sem=ysend_sem.at[k], recv_sem=yrecv_sem.at[k],
            device_id={"ep": xor(me, k, n)}, device_id_type=MESH)

    inner = ((me // 2 + 1) // 2) % 2

    def dispatch(i, _):
        pair, odd = i // 2, i % 2
        first = 1 + 2 * inner
        second = 3 - 2 * inner
        code = ((pair == 0).astype(jnp.int32) * first + (pair == 1).astype(jnp.int32) * second
                + (pair == 2).astype(jnp.int32) * 2)
        k = jnp.where(pair == 3, 1 - odd, 2 * code + odd)
        slot_ids = lax.broadcasted_iota(jnp.int32, (cap, tokens), 0)
        pmat[...] = jnp.where(slot_ids == pos_row[pl.ds(k, 1), :], 1.0, 0.0).astype(bf16)

        def column(c, _):
            cols = pl.ds(pl.multiple_of(c * 512, 512), 512)
            temp[:, cols] = jnp.dot(pmat[...], ubuf[:, cols], preferred_element_type=f32).astype(bf16)
            return 0

        lax.fori_loop(0, ncol, column, 0)

        @pl.when(k == 0)
        def _():
            own = pltpu.make_async_copy(temp, rbuf.at[0], lsem.at[1])
            own.start()
            own.wait()

        @pl.when(k > 0)
        def _():
            stage = pltpu.make_async_copy(temp, sbuf.at[k], lsem.at[1])
            stage.start()
            stage.wait()
            send_copy(k).start()

        return 0

    lax.fori_loop(0, n, dispatch, 0)

    x_copy = pltpu.make_async_copy(x_hbm, ubuf, lsem.at[0])
    x_copy.start()

    def mlp(t, _):
        i, f, slot = t // nf, t % nf, t % 2
        k = visit(i)

        @pl.when(f == 0)
        def _():
            @pl.when(k > 0)
            def _():
                send_copy(k).wait_recv()

            load = pltpu.make_async_copy(rbuf.at[k], xin, lsem.at[1])
            load.start()
            load.wait()
            acc[...] = jnp.zeros_like(acc)

        for c in weight_copies(f, slot):
            c.wait()

        @pl.when(t + 1 < n * nf)
        def _():
            for c in weight_copies((t + 1) % nf, (t + 1) % 2):
                c.start()

        gate_proj = jnp.dot(xin[...], wgb[slot], preferred_element_type=f32)
        up_proj = jnp.dot(xin[...], wub[slot], preferred_element_type=f32)
        inner_act = (jax.nn.silu(gate_proj) * up_proj).astype(bf16)
        for c in range(ncol):
            cols = slice(c * 512, (c + 1) * 512)
            acc[:, cols] += jnp.dot(inner_act, wdb[slot, :, cols], preferred_element_type=f32)

        @pl.when(f == nf - 1)
        def _():
            temp[...] = acc[...].astype(bf16)

            @pl.when(k == 0)
            def _():
                own = pltpu.make_async_copy(temp, bbuf.at[0], lsem.at[1])
                own.start()
                own.wait()

            @pl.when(k > 0)
            def _():
                stage = pltpu.make_async_copy(temp, ybuf.at[k], lsem.at[1])
                stage.start()
                stage.wait()
                back_copy(k).start()

        return 0

    lax.fori_loop(0, n * nf, mlp, 0)
    x_copy.wait()

    def out_copy(r):
        rows = pl.ds(pl.multiple_of(r * tc, tc), tc)
        return pltpu.make_async_copy(ubuf.at[rows, :], out.at[rows, :], osem.at[r])

    def combine(i, _):
        k = visit(i)

        @pl.when(k > 0)
        def _():
            back_copy(k).wait_recv()

        load = pltpu.make_async_copy(bbuf.at[k], xin, lsem.at[1])
        load.start()
        load.wait()

        def rows_step(r, _):
            rows = pl.ds(pl.multiple_of(r * tc, tc), tc)
            lane = lax.broadcasted_iota(jnp.int32, (tc, n), 1)
            pos = jnp.sum(jnp.where(lane == k, pos_col[rows, :], 0), axis=1, keepdims=True)
            gate = jnp.sum(jnp.where(lane == k, gate_col[rows, :], 0.0), axis=1, keepdims=True)
            slot_ids = lax.broadcasted_iota(jnp.int32, (tc, cap), 1)
            pick = jnp.where(slot_ids == pos, 1.0, 0.0).astype(bf16)

            @pl.when(i == 0)
            def _():
                oacc[rows, :] = ubuf[rows, :].astype(f32)

            for c in range(ncol):
                cols = slice(c * 512, (c + 1) * 512)
                picked = jnp.dot(pick, xin[:, cols], preferred_element_type=f32)
                oacc[rows, cols] += gate * picked

            @pl.when(i == n - 1)
            def _():
                ubuf[rows, :] = oacc[rows, :].astype(bf16)
                out_copy(r).start()

            return 0

        lax.fori_loop(0, tokens // tc, rows_step, 0)
        return 0

    lax.fori_loop(0, n, combine, 0)

    def finish(k, _):
        send_copy(k).wait_send()
        back_copy(k).wait_send()
        return 0

    lax.fori_loop(1, n, finish, 0)

    def drain(r, _):
        out_copy(r).wait()
        return 0

    lax.fori_loop(0, tokens // tc, drain, 0)


def solution(mesh):
    group_size = mesh.shape["ep"]
    rows_spec = P(("dp", "ep"))

    def device_step(hidden, ln_gamma, ln_beta, w_router, w_gate, w_up, w_down, choice, mask_first, mask_second):
        tokens, width = hidden.shape
        n = group_size
        ff = w_gate.shape[2]
        cap = (10 * tokens + 4 * n - 1) // (4 * n)
        ft, tc = 512, 256
        normed = layer_norm(hidden, ln_gamma, ln_beta)
        gate_vals = sparse_gates(normed, w_router, choice, mask_first, mask_second)
        experts = lax.axis_index("ep").astype(jnp.int32) ^ jnp.arange(n, dtype=jnp.int32)
        hit = choice[..., None] == experts
        hit_any = jnp.sum(hit.astype(jnp.int32), axis=1)
        before = jnp.cumsum(hit_any, axis=0) - hit_any
        kept = (hit_any > 0) & (before < cap)
        pos = jnp.where(kept, before, -1)
        gates = jnp.where(kept, jnp.sum(jnp.where(hit, gate_vals[..., None], 0.0), axis=1), 0.0)
        block = jax.ShapeDtypeStruct((n, cap, width), jnp.bfloat16)
        vmem = pl.BlockSpec(memory_space=pltpu.VMEM)
        hbm = pl.BlockSpec(memory_space=pl.ANY)
        bf16, f32 = jnp.bfloat16, jnp.float32
        return pl.pallas_call(
            functools.partial(moe_kernel, n, cap, ft, tc),
            out_shape=(jax.ShapeDtypeStruct((tokens, width), bf16), block, block, block, block),
            in_specs=[vmem] * 3 + [hbm] * 5,
            out_specs=(hbm,) * 5,
            scratch_shapes=[
                pltpu.VMEM((tokens, width), bf16),
                pltpu.VMEM((cap, tokens), bf16),
                pltpu.VMEM((cap, width), bf16),
                pltpu.VMEM((cap, width), bf16),
                pltpu.VMEM((cap, width), f32),
                pltpu.VMEM((2, width, ft), bf16),
                pltpu.VMEM((2, width, ft), bf16),
                pltpu.VMEM((2, ft, width), bf16),
                pltpu.VMEM((tokens, width), f32),
                pltpu.SemaphoreType.DMA((n,)),
                pltpu.SemaphoreType.DMA((n,)),
                pltpu.SemaphoreType.DMA((n,)),
                pltpu.SemaphoreType.DMA((n,)),
                pltpu.SemaphoreType.DMA((2, 3)),
                pltpu.SemaphoreType.DMA((2,)),
                pltpu.SemaphoreType.DMA((tokens // tc,)),
            ],
            compiler_params=pltpu.CompilerParams(
                collective_id=0, has_side_effects=True, vmem_limit_bytes=67043328),
            cost_estimate=pl.CostEstimate(
                flops=6 * n * cap * width * ff, bytes_accessed=n * 6 * width * ff, transcendentals=0),
        )(pos.T, pos, gates, normed, hidden, w_gate[0], w_up[0], w_down[0])[0]

    return jax.shard_map(device_step, mesh=mesh,
                         in_specs=(rows_spec, P(), P(), P(), P("ep"), P("ep"), P("ep"), rows_spec, rows_spec, rows_spec),
                         out_specs=rows_spec, check_vma=False)
```

time: 1580 us -> 971 us (0.61)
  Pallas kernels: 0 us -> 931 us
  blocking collectives: 462 us -> 0 us
  waiting for transfers between devices: 446 us -> 0 us
  matrix products: 402 us -> 2.26 us
  local copies, waits for them, and re-layouts: 130 us -> 14.8 us
  other arithmetic: 124 us -> 21.9 us
    pallas_call x0 -> x1, Pallas kernels: none -> 931 us  [device_step(): pl.pallas_call(functools.partial(moe_kernel, n, cap, ft, tc), out_shape=(...]
    all_to_all x1 -> x0, blocking collectives: 462 us -> none  [device_step(): recv_rows = lax.all_to_all(send_rows, 'ep', 0, 0, tiled=True)]
    all_to_all x1 -> x0, waiting for transfers between devices: 446 us -> none  [device_step(): lax.all_to_all(expert_out.reshape(slot_count, row_width), 'ep', 0, 0, til...]
    dot_general x3 -> x0, matrix products: 396 us -> none  [the longest x1 136 us: expert_mlp(): jnp.einsum('secd,edf->secf', expert_in, w_up, preferred_element_type=jnp....]
    gather x3 -> x0, local copies, waits for them, and re-layouts: 111 us -> none  [the longest x2 68 us: device_step(): picked = jnp.take(back_rows, flat_slot, axis=0, mode='fill', fill_value=0)]
    reduce_sum x3 -> x1, other arithmetic: 78.4 us -> 0.08 us  [device_step(): hit_any = jnp.sum(hit.astype(jnp.int32), axis=1)]
  transfers between devices with their start and end apart: 1 -> 0, of which waited for: 1 -> 0; matrix products, arithmetic and copies ran while one was open for 0% -> 0% of each run, Pallas kernels for 0% -> 0%
where the time goes in v1:
time: 971 us; the launch traced here: 970 us
  Pallas kernels  931 us (96%)
  other arithmetic  21.9 us (2%)
  local copies, waits for them, and re-layouts  14.8 us (2%)
    pallas_call x1, Pallas kernels, device_step(): pl.pallas_call(functools.partial(moe_kernel, n, cap, ft, tc), out_shape=(...  931 us

profile of v1, /device:TPU:0, one launch (start us, length us, event | category | flops | bytes accessed | tf_op | source)
XLA Modules:
  0.0 970.3 jit_solution(15861937001806996430)
XLA Ops:
  0.0 0.0 copy-start.2
  0.0 0.0 copy-start.3
  0.0 0.0 copy-start.4
  0.0 4.6 convert_reduce_fusion
  4.6 0.0 copy-start.1
  4.6 5.7 fusion.5
  10.3 0.0 copy-done.2
  10.3 0.1 fusion.19
  10.4 0.4 copy.29
  10.9 0.3 copy.25
  11.2 0.3 copy.26
  11.5 2.5 reduce-window.6
  14.0 0.3 slice_reduce_fusion
  14.3 0.2 reduce-window.9
  14.4 0.1 broadcast_add_fusion
  14.5 0.3 copy.27
  14.9 1.3 fusion.17.pos_col
  16.2 0.2 fusion.15
  16.3 0.9 copy.31.pos_row
  17.3 0.0 copy-done.3
  17.3 0.0 copy-done.4
  17.3 0.0 copy-start.5
  17.3 0.0 copy-start.6
  17.3 6.0 fusion.8.u_hbm
  23.3 0.0 copy-start
  23.3 3.4 copy-done
  26.7 0.0 copy-done.1
  26.7 2.3 fusion.36
  28.9 0.0 copy-done.5
  28.9 0.0 copy-done.6
  28.9 0.1 fusion.33
  29.1 0.3 copy.30
  29.4 1.2 fusion.16.gate_col
  30.6 931.2 %shard_map.100 = (bf16[2048,2048]{1,0:T(8,128)(2,1)}, bf16[8,640,2048]{2,1,0:T(8,128)(2,1)}, bf16[8,640,2048]{2,1,0:T(8,128)(2,1)}, bf16[8,640,2048]{2,1,0:T(8,128)(2,1)}, bf16[8,640,2048]{2,1,0:T(8,128)(2,1)}) custom-call(s32[8,2048]{1,0:T(8,128)} %copy.31.pos_row, s32[2048,8]{1,0:T(8,128)} %fusion.17.pos_col, f32[2048,8]{1,0:T(8,128)} %fusion.16.gate_col, ...), custom_call_target="tpu_custom_call" | custom-call | flops 354334801920 | bytes 553648128 | tf_op jit(solution)/shard_map/pallas_call | solution.py:256
  961.9 8.4 copy.33
  (4 shorter events, 0.0 us)
Async XLA Ops:
  0.0 10.3 %copy-start.2 = (s32[2048,2]{0,1:T(2,128)S(1)}, s32[2048,2]{0,1:T(2,128)}, u32[]{:S(2)}) copy-start(s32[2048,2]{0,1:T(2,128)} %param.17) | copy-start | bytes 49156
  0.0 17.3 %copy-start.3 = (f32[2048]{0:T(1024)S(1)}, f32[2048]{0:T(1024)}, u32[]{:S(2)}) copy-start(f32[2048]{0:T(1024)} %param.12) | copy-start | bytes 24580
  0.0 17.3 %copy-start.4 = (f32[2048]{0:T(1024)S(1)}, f32[2048]{0:T(1024)}, u32[]{:S(2)}) copy-start(f32[2048]{0:T(1024)} %param.11) | copy-start | bytes 24580
  4.6 22.1 %copy-start.1 = (bf16[2048,8]{0,1:T(8,128)(2,1)S(1)}, bf16[2048,8]{0,1:T(8,128)(2,1)}, u32[]{:S(2)}) copy-start(bf16[2048,8]{0,1:T(8,128)(2,1)} %param.13) | copy-start | bytes 98308
  17.3 11.7 %copy-start.5 = (s32[2048,8]{0,1:T(8,128)S(1)}, s32[2048,8]{0,1:T(8,128)}, u32[]{:S(2)}) copy-start(s32[2048,8]{0,1:T(8,128)} %param.19) | copy-start | bytes 196612
  17.3 11.7 %copy-start.6 = (s32[2048,8]{0,1:T(8,128)S(1)}, s32[2048,8]{0,1:T(8,128)}, u32[]{:S(2)}) copy-start(s32[2048,8]{0,1:T(8,128)} %param.18) | copy-start | bytes 196612
  23.3 3.4 copy-start

commit v2 on v1

--- a/solution.py
+++ b/solution.py
@@ -35,19 +35,22 @@
     return total
 
 
-def visit(i):
-    return i + (i // 4) * (2 - 4 * ((i // 2) % 2))
-
-
 def moe_kernel(n, cap, ft, tc, pos_row, pos_col, gate_col, u_hbm, x_hbm, wg, wu, wd,
-               out, sbuf, rbuf, ybuf, bbuf,
-               ubuf, pmat, temp, xin, acc, wgb, wub, wdb, oacc,
-               send_sem, recv_sem, ysend_sem, yrecv_sem, wsem, lsem, osem):
+               out, sbuf, rbuf, ybuf, bbuf, ufar, fbuf,
+               ubuf, pmat, temp, xin, acc, wgb, wub, wdb, oacc, posfar,
+               send_sem, recv_sem, ysend_sem, yrecv_sem, usend_sem, urecv_sem, fsend_sem, wsem, lsem, osem, go_sem):
     me = lax.axis_index("ep")
     tokens, width = ubuf.shape
     nf = wg.shape[1] // ft
     ncol = width // 512
     bf16, f32 = jnp.bfloat16, jnp.float32
+    inner = ((me // 2 + 1) // 2) % 2
+
+    def visit(i):
+        return i + inner * (i // 4) * (2 - 4 * ((i // 2) % 2))
+
+    def gather_back(i):
+        return i + (1 - inner) * (i // 4) * (2 - 4 * ((i // 2) % 2))
 
     u_copy = pltpu.make_async_copy(u_hbm, ubuf, lsem.at[0])
     u_copy.start()
@@ -69,6 +72,22 @@
 
     lax.fori_loop(1, n, greet, 0)
     pl.semaphore_wait(barrier, n - 1)
+
+    def far_rows(slot):
+        return pltpu.make_async_remote_copy(
+            src_ref=u_hbm, dst_ref=ufar.at[slot], send_sem=usend_sem.at[0], recv_sem=urecv_sem.at[slot, 0],
+            device_id={"ep": xor(me, 4 + 2 * inner, n)}, device_id_type=MESH)
+
+    def far_slots(slot):
+        return pltpu.make_async_remote_copy(
+            src_ref=pos_row, dst_ref=posfar.at[slot], send_sem=usend_sem.at[1], recv_sem=urecv_sem.at[slot, 1],
+            device_id={"ep": xor(me, 4 + 2 * inner, n)}, device_id_type=MESH)
+
+    @pl.when(inner == 1)
+    def _():
+        far_rows(0).start()
+
+    far_slots(1 - inner).start()
     u_copy.wait()
 
     def send_copy(k):
@@ -76,22 +95,25 @@
             src_ref=sbuf.at[k], dst_ref=rbuf.at[k], send_sem=send_sem.at[k], recv_sem=recv_sem.at[k],
             device_id={"ep": xor(me, k, n)}, device_id_type=MESH)
 
+    def forward_copy(slot, j):
+        k = xor(6 - 2 * slot, j, n)
+        return pltpu.make_async_remote_copy(
+            src_ref=fbuf.at[slot, j], dst_ref=rbuf.at[k], send_sem=fsend_sem.at[slot, j], recv_sem=recv_sem.at[k],
+            device_id={"ep": xor(me, j, n)}, device_id_type=MESH)
+
     def back_copy(k):
         return pltpu.make_async_remote_copy(
             src_ref=ybuf.at[k], dst_ref=bbuf.at[k], send_sem=ysend_sem.at[k], recv_sem=yrecv_sem.at[k],
             device_id={"ep": xor(me, k, n)}, device_id_type=MESH)
 
-    inner = ((me // 2 + 1) // 2) % 2
-
-    def dispatch(i, _):
-        pair, odd = i // 2, i % 2
-        first = 1 + 2 * inner
-        second = 3 - 2 * inner
-        code = ((pair == 0).astype(jnp.int32) * first + (pair == 1).astype(jnp.int32) * second
-                + (pair == 2).astype(jnp.int32) * 2)
-        k = jnp.where(pair == 3, 1 - odd, 2 * code + odd)
+    def put(dst):
+        c = pltpu.make_async_copy(temp, dst, lsem.at[1])
+        c.start()
+        c.wait()
+
+    def gather(positions):
         slot_ids = lax.broadcasted_iota(jnp.int32, (cap, tokens), 0)
-        pmat[...] = jnp.where(slot_ids == pos_row[pl.ds(k, 1), :], 1.0, 0.0).astype(bf16)
+        pmat[...] = jnp.where(slot_ids == positions, 1.0, 0.0).astype(bf16)
 
         def column(c, _):
             cols = pl.ds(pl.multiple_of(c * 512, 512), 512)
@@ -100,35 +122,79 @@
 
         lax.fori_loop(0, ncol, column, 0)
 
+    def dispatch(i, _):
+        k = 2 - i + (i // 2) * (5 - i - (i // 3))
+        gather(pos_row[pl.ds(k, 1), :])
+
         @pl.when(k == 0)
         def _():
-            own = pltpu.make_async_copy(temp, rbuf.at[0], lsem.at[1])
-            own.start()
-            own.wait()
+            put(rbuf.at[0])
 
         @pl.when(k > 0)
         def _():
-            stage = pltpu.make_async_copy(temp, sbuf.at[k], lsem.at[1])
-            stage.start()
-            stage.wait()
+            put(sbuf.at[k])
             send_copy(k).start()
 
         return 0
 
-    lax.fori_loop(0, n, dispatch, 0)
-
-    x_copy = pltpu.make_async_copy(x_hbm, ubuf, lsem.at[0])
-    x_copy.start()
+    lax.fori_loop(0, 4, dispatch, 0)
+
+    def forward(slot):
+        far_rows(slot).wait_recv()
+        far_slots(slot).wait_recv()
+        load = pltpu.make_async_copy(ufar.at[slot], ubuf, lsem.at[0])
+        load.start()
+        load.wait()
+
+        def target(i, _):
+            j = 2 - i + (i // 2) * (5 - i - (i // 3))
+            k = xor(6 - 2 * slot, j, n)
+            gather(posfar[slot, pl.ds(k, 1), :])
+
+            @pl.when(j == 0)
+            def _():
+                put(rbuf.at[k])
+
+            @pl.when(j > 0)
+            def _():
+                put(fbuf.at[slot, j])
+                forward_copy(slot, j).start()
+
+            return 0
+
+        lax.fori_loop(0, 4, target, 0)
 
     def mlp(t, _):
         i, f, slot = t // nf, t % nf, t % 2
         k = visit(i)
 
+        @pl.when((f == 0) & (inner == 0) & (i == 3))
+        def _():
+            pl.semaphore_wait(go_sem, 2)
+            far_rows(1).start()
+
+        @pl.when((f == 0) & (inner == 1) & (i == 3))
+        def _():
+            far_rows(0).wait_send()
+            for j in (2, 3):
+                pl.semaphore_signal(go_sem, inc=1, device_id={"ep": xor(me, j, n)}, device_id_type=MESH)
+
+        @pl.when((f == 0) & (inner == 1) & (i % 3 == 0) & (i > 0))
+        def _():
+            forward(i // 3 - 1)
+
+            @pl.when(i == 6)
+            def _():
+                back_copy(7).start()
+
         @pl.when(f == 0)
         def _():
-            @pl.when(k > 0)
-            def _():
-                send_copy(k).wait_recv()
+            @pl.when((k > 0) & ((inner == 0) | (k < 4) | (k % 2 == 1)))
+            def _():
+                back_copy_like = pltpu.make_async_remote_copy(
+                    src_ref=ybuf.at[k], dst_ref=rbuf.at[k], send_sem=send_sem.at[0], recv_sem=recv_sem.at[k],
+                    device_id={"ep": xor(me, k, n)}, device_id_type=MESH)
+                back_copy_like.wait_recv()
 
             load = pltpu.make_async_copy(rbuf.at[k], xin, lsem.at[1])
             load.start()
@@ -156,20 +222,21 @@
 
             @pl.when(k == 0)
             def _():
-                own = pltpu.make_async_copy(temp, bbuf.at[0], lsem.at[1])
-                own.start()
-                own.wait()
+                put(bbuf.at[0])
 
             @pl.when(k > 0)
             def _():
-                stage = pltpu.make_async_copy(temp, ybuf.at[k], lsem.at[1])
-                stage.start()
-                stage.wait()
+                put(ybuf.at[k])
+
+            @pl.when((k > 0) & ((inner == 0) | (i != 5)))
+            def _():
                 back_copy(k).start()
 
         return 0
 
     lax.fori_loop(0, n * nf, mlp, 0)
+    x_copy = pltpu.make_async_copy(x_hbm, ubuf, lsem.at[0])
+    x_copy.start()
     x_copy.wait()
 
     def out_copy(r):
@@ -177,7 +244,7 @@
         return pltpu.make_async_copy(ubuf.at[rows, :], out.at[rows, :], osem.at[r])
 
     def combine(i, _):
-        k = visit(i)
+        k = gather_back(i)
 
         @pl.when(k > 0)
         def _():
@@ -217,11 +284,26 @@
     lax.fori_loop(0, n, combine, 0)
 
     def finish(k, _):
-        send_copy(k).wait_send()
         back_copy(k).wait_send()
+
+        @pl.when(k < 4)
+        def _():
+            send_copy(k).wait_send()
+
+        @pl.when((k < 4) & (inner == 1))
+        def _():
+            forward_copy(0, k).wait_send()
+            forward_copy(1, k).wait_send()
+
         return 0
 
     lax.fori_loop(1, n, finish, 0)
+    far_slots(0).wait_send()
+
+    @pl.when(inner == 0)
+    def _():
+        far_rows(0).wait_send()
+
 
     def drain(r, _):
         out_copy(r).wait()
@@ -250,14 +332,17 @@
         pos = jnp.where(kept, before, -1)
         gates = jnp.where(kept, jnp.sum(jnp.where(hit, gate_vals[..., None], 0.0), axis=1), 0.0)
         block = jax.ShapeDtypeStruct((n, cap, width), jnp.bfloat16)
+        near = jax.ShapeDtypeStruct((n // 2, cap, width), jnp.bfloat16)
+        far_rows = jax.ShapeDtypeStruct((2, tokens, width), jnp.bfloat16)
+        far_blocks = jax.ShapeDtypeStruct((2, n // 2, cap, width), jnp.bfloat16)
         vmem = pl.BlockSpec(memory_space=pltpu.VMEM)
         hbm = pl.BlockSpec(memory_space=pl.ANY)
         bf16, f32 = jnp.bfloat16, jnp.float32
         return pl.pallas_call(
             functools.partial(moe_kernel, n, cap, ft, tc),
-            out_shape=(jax.ShapeDtypeStruct((tokens, width), bf16), block, block, block, block),
+            out_shape=(jax.ShapeDtypeStruct((tokens, width), bf16), near, block, block, block, far_rows, far_blocks),
             in_specs=[vmem] * 3 + [hbm] * 5,
-            out_specs=(hbm,) * 5,
+            out_specs=(hbm,) * 7,
             scratch_shapes=[
                 pltpu.VMEM((tokens, width), bf16),
                 pltpu.VMEM((cap, tokens), bf16),
@@ -268,13 +353,18 @@
                 pltpu.VMEM((2, width, ft), bf16),
                 pltpu.VMEM((2, ft, width), bf16),
                 pltpu.VMEM((tokens, width), f32),
+                pltpu.VMEM((2, n, tokens), jnp.int32),
                 pltpu.SemaphoreType.DMA((n,)),
                 pltpu.SemaphoreType.DMA((n,)),
                 pltpu.SemaphoreType.DMA((n,)),
                 pltpu.SemaphoreType.DMA((n,)),
+                pltpu.SemaphoreType.DMA((2,)),
+                pltpu.SemaphoreType.DMA((2, 2)),
+                pltpu.SemaphoreType.DMA((2, n // 2)),
                 pltpu.SemaphoreType.DMA((2, 3)),
                 pltpu.SemaphoreType.DMA((2,)),
                 pltpu.SemaphoreType.DMA((tokens // tc,)),
+                pltpu.SemaphoreType.REGULAR,
             ],
             compiler_params=pltpu.CompilerParams(
                 collective_id=0, has_side_effects=True, vmem_limit_bytes=67043328),

time: 971 us -> 936 us (0.964)
  Pallas kernels: 931 us -> 897 us
    pallas_call x1, Pallas kernels: 931 us -> 897 us  [device_step(): pl.pallas_call(functools.partial(moe_kernel, n, cap, ft, tc), out_shape=(...]
where the time goes in v2:
time: 936 us
  Pallas kernels  897 us (96%)
  other arithmetic  21.8 us (2%)
  local copies, waits for them, and re-layouts  14.8 us (2%)
    pallas_call x1, Pallas kernels, device_step(): pl.pallas_call(functools.partial(moe_kernel, n, cap, ft, tc), out_shape=(...  897 us

profile of v2, /device:TPU:0, one launch (start us, length us, event | category | flops | bytes accessed | tf_op | source)
XLA Modules:
  0.0 935.6 jit_solution(987466114719857066)
XLA Ops:
  0.0 0.0 copy-start.2
  0.0 0.0 copy-start.3
  0.0 0.0 copy-start.4
  0.0 4.6 convert_reduce_fusion
  4.6 0.0 copy-start.1
  4.6 5.7 fusion.5
  10.3 0.0 copy-done.2
  10.3 0.1 fusion.19
  10.4 0.4 copy.29
  10.9 0.3 copy.25
  11.2 0.3 copy.26
  11.5 2.5 reduce-window.6
  14.0 0.3 slice_reduce_fusion
  14.3 0.2 reduce-window.9
  14.4 0.1 broadcast_add_fusion
  14.5 0.3 copy.27
  14.9 1.3 fusion.17.pos_col
  16.1 0.2 fusion.15
  16.3 0.9 copy.31.pos_row
  17.2 0.0 copy-done.3
  17.2 0.0 copy-done.4
  17.2 0.0 copy-start.5
  17.2 0.0 copy-start.6
  17.2 6.0 fusion.8.u_hbm
  23.2 0.0 copy-start
  23.2 3.4 copy-done
  26.6 0.0 copy-done.1
  26.6 2.3 fusion.36
  28.9 0.0 copy-done.5
  28.9 0.0 copy-done.6
  28.9 0.1 fusion.33
  29.0 0.3 copy.30
  29.4 1.2 fusion.16.gate_col
  30.6 896.6 %shard_map.100 = (bf16[2048,2048]{1,0:T(8,128)(2,1)}, bf16[4,640,2048]{2,1,0:T(8,128)(2,1)}, bf16[8,640,2048]{2,1,0:T(8,128)(2,1)}, bf16[8,640,2048]{2,1,0:T(8,1...) custom-call(s32[8,2048]{1,0:T(8,128)} %copy.31.pos_row, ...), custom_call_target="tpu_custom_call" | custom-call | flops 354334801920 | bytes 553648128 | tf_op jit(solution)/shard_map/pallas_call | solution.py:341
  927.2 8.4 copy.33
  (4 shorter events, 0.0 us)
Async XLA Ops:
  0.0 10.3 %copy-start.2 = (s32[2048,2]{0,1:T(2,128)S(1)}, s32[2048,2]{0,1:T(2,128)}, u32[]{:S(2)}) copy-start(s32[2048,2]{0,1:T(2,128)} %param.17) | copy-start | bytes 49156
  0.0 17.2 %copy-start.3 = (f32[2048]{0:T(1024)S(1)}, f32[2048]{0:T(1024)}, u32[]{:S(2)}) copy-start(f32[2048]{0:T(1024)} %param.12) | copy-start | bytes 24580
  0.0 17.2 %copy-start.4 = (f32[2048]{0:T(1024)S(1)}, f32[2048]{0:T(1024)}, u32[]{:S(2)}) copy-start(f32[2048]{0:T(1024)} %param.11) | copy-start | bytes 24580
  4.6 22.0 %copy-start.1 = (bf16[2048,8]{0,1:T(8,128)(2,1)S(1)}, bf16[2048,8]{0,1:T(8,128)(2,1)}, u32[]{:S(2)}) copy-start(bf16[2048,8]{0,1:T(8,128)(2,1)} %param.13) | copy-start | bytes 98308
  17.2 11.7 %copy-start.5 = (s32[2048,8]{0,1:T(8,128)S(1)}, s32[2048,8]{0,1:T(8,128)}, u32[]{:S(2)}) copy-start(s32[2048,8]{0,1:T(8,128)} %param.19) | copy-start | bytes 196612
  17.2 11.7 %copy-start.6 = (s32[2048,8]{0,1:T(8,128)S(1)}, s32[2048,8]{0,1:T(8,128)}, u32[]{:S(2)}) copy-start(s32[2048,8]{0,1:T(8,128)} %param.18) | copy-start | bytes 196612
  23.2 3.4 copy-start

commit v3 on v2

--- a/solution.py
+++ b/solution.py
@@ -11,11 +11,26 @@
 MESH = pl.DeviceIdType.MESH
 
 
-def layer_norm(token_rows, ln_gamma, ln_beta):
-    values = token_rows.astype(jnp.float32)
+def norm_kernel(x_ref, gamma_ref, beta_ref, out_ref):
+    values = x_ref[...].astype(jnp.float32)
     centred = values - jnp.mean(values, axis=-1, keepdims=True)
     variance = jnp.mean(centred * centred, axis=-1, keepdims=True)
-    return (centred * lax.rsqrt(variance + LN_EPS) * ln_gamma + ln_beta).astype(jnp.bfloat16)
+    out_ref[...] = (centred * lax.rsqrt(variance + LN_EPS) * gamma_ref[...] + beta_ref[...]).astype(jnp.bfloat16)
+
+
+def layer_norm(token_rows, ln_gamma, ln_beta):
+    tokens, width = token_rows.shape
+    rows = pl.BlockSpec((256, width), lambda i: (i, 0))
+    whole = pl.BlockSpec((1, width), lambda i: (0, 0))
+    return pl.pallas_call(
+        norm_kernel,
+        grid=(tokens // 256,),
+        out_shape=jax.ShapeDtypeStruct((tokens, width), jnp.bfloat16),
+        in_specs=[rows, whole, whole],
+        out_specs=rows,
+        compiler_params=pltpu.CompilerParams(vmem_limit_bytes=32 << 20),
+        cost_estimate=pl.CostEstimate(flops=8 * tokens * width, bytes_accessed=4 * tokens * width, transcendentals=tokens),
+    )(token_rows, ln_gamma[None, :], ln_beta[None, :])
 
 
 def sparse_gates(normed, w_router, choice, mask_first, mask_second):

time: 936 us -> 933 us (level)
  other arithmetic: 21.8 us -> 7.04 us
    reduce_sum x2 -> x0, other arithmetic: 10.3 us -> none  [the longest x1 5.69 us: layer_norm(): variance = jnp.mean(centred * centred, axis=-1, keepdims=True)]
where the time goes in v3:
time: 933 us; the launch traced here: 932 us
  Pallas kernels  903 us (97%)
  local copies, waits for them, and re-layouts  19.6 us (2%)
    pallas_call x1, Pallas kernels, device_step(): pl.pallas_call(functools.partial(moe_kernel, n, cap, ft, tc), out_shape=(...  897 us

profile of v3, /device:TPU:0, one launch (start us, length us, event | category | flops | bytes accessed | tf_op | source)
XLA Modules:
  0.0 931.6 jit_solution(12984705014592396203)
XLA Ops:
  0.0 0.0 copy-start.4
  0.0 0.8 fusion.13
  0.8 0.4 copy.29
  1.3 0.3 copy.25
  1.6 0.3 copy.26
  1.9 2.3 reduce-window.6
  4.2 0.3 slice_reduce_fusion
  4.5 0.2 reduce-window.9
  4.7 0.1 broadcast_add_fusion
  4.8 0.3 copy.27
  5.1 1.3 fusion.11.pos_col
  6.4 0.0 copy-start.5
  6.4 0.2 fusion.9
  6.5 0.9 copy.31.pos_row
  7.5 0.0 copy-start.1
  7.5 3.4 copy-done.1
  10.8 0.0 copy-start.2
  10.8 0.7 copy-done.2
  11.5 0.0 copy-start.3
  11.5 0.7 copy-done.3
  12.2 6.1 shard_map.100.u_hbm
  18.3 0.0 copy-start
  18.3 3.4 copy-done
  21.7 0.0 copy-done.4
  21.7 2.3 fusion.30
  24.0 0.0 copy-done.5
  24.0 1.0 fusion.27
  25.0 0.3 copy.30
  25.4 1.2 fusion.10.gate_col
  26.6 896.6 %shard_map.101 = (bf16[2048,2048]{1,0:T(8,128)(2,1)}, bf16[4,640,2048]{2,1,0:T(8,128)(2,1)}, bf16[8,640,2048]{2,1,0:T(8,128)(2,1)}, bf16[8,640,2048]{2,1,0:T(8,1...) custom-call(s32[8,2048]{1,0:T(8,128)} %copy.31.pos_row, ...), custom_call_target="tpu_custom_call" | custom-call | flops 354334801920 | bytes 553648128 | tf_op jit(solution)/shard_map/pallas_call | solution.py:356
  923.1 8.4 copy.33
  (2 shorter events, 0.0 us)
Async XLA Ops:
  0.0 21.7 %copy-start.4 = (bf16[2048,8]{0,1:T(8,128)(2,1)S(1)}, bf16[2048,8]{0,1:T(8,128)(2,1)}, u32[]{:S(2)}) copy-start(bf16[2048,8]{0,1:T(8,128)(2,1)} %param.13) | copy-start | bytes 98308
  6.4 17.6 %copy-start.5 = (s32[2048,2]{0,1:T(2,128)S(1)}, s32[2048,2]{0,1:T(2,128)}, u32[]{:S(2)}) copy-start(s32[2048,2]{0,1:T(2,128)} %param.17) | copy-start | bytes 49156
  7.5 3.4 copy-start.1
  10.8 0.7 copy-start.2
  11.5 0.7 copy-start.3
  18.3 3.4 copy-start
